TPU v7x, 32 devices: a whole 2x2x4 slice. The times are simulated.
32 devices in a mesh: gx: 4 (over x, core), gy: 8 (over z, y).
Axes of the slice: x: 2, y: 2, z: 4, core: 2. Of those that a mesh axis runs over, the one named last changes fastest.
Arguments:
- substrate: float32 [16, 64, 1024], P(None, 'gy', 'gx'), may hold values from 0 to 1
- catalyst: float32 [16, 64, 1024], P(None, 'gy', 'gx'), may hold values from 0 to 1
Outputs:
- substrate_next: float32 [16, 64, 1024], P(None, 'gy', 'gx')
- catalyst_next: float32 [16, 64, 1024], P(None, 'gy', 'gx')
- rebuilt: float32 [2, 16, 1024, 64], P(None, None, ('gx', 'gy'))
All inputs are finite; a program needn't handle non-finite values.
Results may differ from a plain program's by a relative error of at most 0.00002.
Values sent between devices are 32-bit elements; how exact they have to be, the bound alone decides.
A program may use at most 64 MiB of HBM per device.

v0:
```python
import jax
import jax.numpy as jnp
from jax import lax
from jax.sharding import PartitionSpec as P

feed_rate = 0.037
kill_rate = 0.06
substrate_diffusion = 0.15
catalyst_diffusion = 0.08


def with_halo(shard, sides, width):
    for axis, dim in sides:
        size, length = (lax.axis_size(axis), shard.shape[dim])
        up = [(i, (i + 1) % size) for i in range(size)]
        down = [(j, i) for i, j in up]
        last = lax.slice_in_dim(shard, length - width, length, axis=dim)
        first = lax.slice_in_dim(shard, 0, width, axis=dim)
        before = lax.ppermute(last, axis, up)
        after = lax.ppermute(first, axis, down)
        shard = jnp.concatenate([before, shard, after], axis=dim)
    return shard


def react(center, spread):
    substrate = center[0]
    catalyst = center[1]
    reaction = substrate * catalyst * catalyst
    new_substrate = (
        substrate + substrate_diffusion * spread[0] - reaction + feed_rate * (1.0 - substrate)
    )
    new_catalyst = (
        catalyst + catalyst_diffusion * spread[1] + reaction - (feed_rate + kill_rate) * catalyst
    )
    return jnp.stack([new_substrate, new_catalyst])


def advance(padded):
    center = padded[:, :, 1:-1, 1:-1]
    spread = jnp.roll(center, 1, 1) + jnp.roll(center, -1, 1)
    spread = spread + padded[:, :, 2:, 1:-1] + padded[:, :, :-2, 1:-1]
    spread = spread + padded[:, :, 1:-1, 2:] + padded[:, :, 1:-1, :-2]
    return react(center, spread - 6.0 * center)


def restrict(field):
    shape = field.shape
    blocks = field.reshape(shape[0], shape[1], shape[2] // 2, 2, shape[3] // 2, 2)
    return (
        blocks[:, :, :, 0, :, 0]
        + blocks[:, :, :, 0, :, 1]
        + blocks[:, :, :, 1, :, 0]
        + blocks[:, :, :, 1, :, 1]
    ) * 0.25


def prolong(field):
    return jnp.repeat(jnp.repeat(field, 2, axis=2), 2, axis=3)


def pack(level, owners):
    fields, planes, extent, columns = level.shape
    portion = columns // owners
    blocks = level.reshape(fields, planes, extent, owners, portion)
    blocks = jnp.transpose(blocks, (0, 3, 1, 4, 2))
    return blocks.reshape(fields, owners, planes * portion * extent)


def unpack(received, shape, owners):
    fields, planes, extent, columns = shape
    portion = columns // owners
    blocks = received.reshape(fields, owners, planes, portion, extent)
    blocks = jnp.transpose(blocks, (0, 2, 3, 1, 4))
    return blocks.reshape(fields, planes, portion, owners * extent)


def body(substrate, catalyst):
    state = jnp.stack([substrate, catalyst])
    padded = with_halo(state, (("gx", 3), ("gy", 2)), 2)
    state = advance(advance(padded))
    level1 = restrict(state)
    level2 = restrict(level1)
    owners = lax.axis_size("gy")
    detail = level1 - prolong(level2)
    got_detail, got_coarse = (
        lax.all_to_all(pack(detail, owners), "gy", split_axis=1, concat_axis=1, tiled=True),
        lax.all_to_all(pack(level2, owners), "gy", split_axis=1, concat_axis=1, tiled=True),
    )
    coarse = prolong(unpack(got_coarse, level2.shape, owners))
    blend = coarse + 0.5 * unpack(got_detail, level1.shape, owners)
    rebuilt = prolong(blend)
    return (state[0], state[1], rebuilt)


def solution(mesh):
    in_specs = (P(None, "gy", "gx"), P(None, "gy", "gx"))
    out_specs = (P(None, "gy", "gx"), P(None, "gy", "gx"), P(None, None, ("gx", "gy"), None))
    return jax.shard_map(body, mesh=mesh, in_specs=in_specs, out_specs=out_specs, check_vma=False)
```

profile of v0, /device:TPU:0, one launch (start us, length us, event | category | flops | bytes accessed | tf_op | source)
XLA Modules:
  0.0 48.9 jit_solution(7610044865911869305)
XLA Ops:
  0.6 1.1 %fusion.26 = (f32[2,16,8,2]{3,2,1,0:T(8,128)S(1)}, f32[2,16,8,2]{3,2,1,0:T(8,128)S(1)}) fusion(f32[1,16,8,256]{3,2,1,0:T(8,128)} %bitcast.75, f32[1,16,8,256]{3,2,1,0:T(8,128)} %bitcast.79), kind=kLoop, calls=%fused_computation.78 | loop fusion | flops 1024 | bytes 266240 | tf_op jit(solution)/shard_map/stack | solution.py:78
  1.7 0.5 %collective-permute-start = (f32[2,16,8,2]{3,2,1,0:T(8,128)S(1)}, f32[2,16,8,2]{3,2,1,0:T(8,128)S(1)}, u32[]{:S(2)}, u32[]{:S(2)}) collective-permute-start(f32[2,16,8,2]{3,2,1,0:T(8,128)S(1)} %get-tuple-element.27), channel_id=1, source_target_pairs={{0,8},{8,16},{16,24},{24,0},{1,9},{9,17},{17,25},{25,1},{2,10},{10... | collective-permute-start | bytes 6152 | tf_op jit(solution)/shard_map/ppermute | solution.py:19
  2.3 2.0 %collective-permute-start.1 = (f32[2,16,8,2]{3,2,1,0:T(8,128)S(1)}, f32[2,16,8,2]{3,2,1,0:T(8,128)S(1)}, u32[]{:S(2)}, u32[]{:S(2)}) collective-permute-start(f32[2,16,8,2]{3,2,1,0:T(8,128)S(1)} %get-tuple-element.28), channel_id=1, source_target_pairs={{8,0},{16,8},{24,16},{0,24},{9,1},{17,9},{25,17},{1,25},{10,2},{18... | collective-permute-start | bytes 6152 | tf_op jit(solution)/shard_map/ppermute | solution.py:20
  4.2 2.6 %collective-permute-done = f32[2,16,8,2]{3,2,1,0:T(8,128)S(1)} collective-permute-done((f32[2,16,8,2]{3,2,1,0:T(8,128)S(1)}, f32[2,16,8,2]{3,2,1,0:T(8,128)S(1)}, u32[]{:S(2)}, u32[]{:S(2)}) %collective-permute-start) | collective-permute-done | bytes 2080 | tf_op jit(solution)/shard_map/ppermute | solution.py:19
  6.8 1.2 %collective-permute-done.1 = f32[2,16,8,2]{3,2,1,0:T(8,128)S(1)} collective-permute-done((f32[2,16,8,2]{3,2,1,0:T(8,128)S(1)}, f32[2,16,8,2]{3,2,1,0:T(8,128)S(1)}, u32[]{:S(2)}, u32[]{:S(2)}) %collective-permute-start.1) | collective-permute-done | bytes 2080 | tf_op jit(solution)/shard_map/ppermute | solution.py:20
  8.4 1.6 %collective-permute-start.2 = (f32[2,16,2,260]{3,2,1,0:T(2,128)S(1)}, f32[2,16,2,260]{3,2,1,0:T(2,128)S(1)}, u32[]{:S(2)}, u32[]{:S(2)}) collective-permute-start(f32[2,16,2,260]{3,2,1,0:T(2,128)S(1)} %get-tuple-element.25), channel_id=1, source_target_pairs={{0,1},{1,2},{2,3},{3,4},{4,5},{5,6},{6,7},{7,0},{8,9},{9,10},{10,1... | collective-permute-start | bytes 199688 | tf_op jit(solution)/shard_map/ppermute | solution.py:19
  10.0 3.2 %collective-permute-start.3 = (f32[2,16,2,260]{3,2,1,0:T(2,128)S(1)}, f32[2,16,2,260]{3,2,1,0:T(2,128)S(1)}, u32[]{:S(2)}, u32[]{:S(2)}) collective-permute-start(f32[2,16,2,260]{3,2,1,0:T(2,128)S(1)} %get-tuple-element.26), channel_id=1, source_target_pairs={{1,0},{2,1},{3,2},{4,3},{5,4},{6,5},{7,6},{0,7},{9,8},{10,9},{11,1... | collective-permute-start | bytes 199688 | tf_op jit(solution)/shard_map/ppermute | solution.py:20
  13.2 3.4 %collective-permute-done.2 = f32[2,16,2,260]{3,2,1,0:T(2,128)S(1)} collective-permute-done((f32[2,16,2,260]{3,2,1,0:T(2,128)S(1)}, f32[2,16,2,260]{3,2,1,0:T(2,128)S(1)}, u32[]{:S(2)}, u32[]{:S(2)}) %collective-permute-start.2) | collective-permute-done | bytes 66592 | tf_op jit(solution)/shard_map/ppermute | solution.py:19
  16.6 1.1 %collective-permute-done.3 = f32[2,16,2,260]{3,2,1,0:T(2,128)S(1)} collective-permute-done((f32[2,16,2,260]{3,2,1,0:T(2,128)S(1)}, f32[2,16,2,260]{3,2,1,0:T(2,128)S(1)}, u32[]{:S(2)}, u32[]{:S(2)}) %collective-permute-start.3) | collective-permute-done | bytes 66592 | tf_op jit(solution)/shard_map/ppermute | solution.py:20
  18.1 0.5 fusion.41
  18.5 1.3 %fusion = f32[2,16,10,258]{3,2,1,0:T(8,128)S(1)} fusion(f32[2,16,12,260]{3,2,1,0:T(8,128)S(1)} %pad_maximum_fusion.18, f32[2,16,2,260]{3,2,1,0:T(2,128)S(1)} %collective-permute-done.2, f32[2,16,8,2]{3,2,1,0:T(8,128)S(1)} %collective-permute-done.1, f32[2,16,8,2]{3,2,1,0:T(8,128)S(1)} %collective-permute-done, f32[1,16,8,256]{3,2,1,0:T(8,128)S(1)} %bitcast.82, ...), kind=kLoop, calls=%fused_computation.15 | loop fusion | flops 2229120 | bytes 2339520 | tf_op jit(solution)/shard_map/sub | solution.py:43
  21.3 0.4 copy.56
  21.7 0.4 copy.53
  22.1 0.4 copy.55
  23.4 0.7 %copy.59 = f32[2,8,256]{2,0,1:T(2,128)} copy(f32[2,8,256]{1,2,0:T(8,128)S(1)} %bitcast.88) | data formatting | bytes 32768 | tf_op jit(solution)/shard_map/reshape | solution.py:66
  24.1 5.0 %all-to-all-start = ((f32[2,8,256]{2,0,1:T(2,128)}), f32[2,8,256]{2,0,1:T(2,128)S(1)}, u32[]{:S(2)}, u32[]{:S(2)}) async-start(f32[2,8,256]{2,0,1:T(2,128)} %copy.59), calls=%async_computation | async-start | bytes 32768 | tf_op jit(solution)/shard_map/all_to_all | solution.py:87
  29.7 0.4 copy.67
  30.1 0.9 %copy.68 = f32[2,8,1024]{2,0,1:T(2,128)} copy(f32[2,8,1024]{1,2,0:T(8,128)S(1)} %bitcast.68) | data formatting | bytes 131072 | tf_op jit(solution)/shard_map/reshape | solution.py:66
  31.0 4.7 %all-to-all-done = f32[2,8,256]{2,0,1:T(2,128)S(1)} async-done(((f32[2,8,256]{2,0,1:T(2,128)}), f32[2,8,256]{2,0,1:T(2,128)S(1)}, u32[]{:S(2)}, u32[]{:S(2)}) %all-to-all-start) | async-done | bytes 16416 | tf_op jit(solution)/shard_map/all_to_all | solution.py:87
  35.7 3.4 %all-to-all-start.1 = ((f32[2,8,1024]{2,0,1:T(2,128)}), f32[2,8,1024]{2,0,1:T(2,128)S(1)}, u32[]{:S(2)}, u32[]{:S(2)}) async-start(f32[2,8,1024]{2,0,1:T(2,128)} %copy.68), calls=%async_computation.1 | async-start | bytes 131072 | tf_op jit(solution)/shard_map/all_to_all | solution.py:86
  39.1 0.8 %fusion.29 = (f32[16,8,256]{2,1,0:T(8,128)}, f32[16,8,256]{2,1,0:T(8,128)}) fusion(f32[2,16,8,256]{3,2,1,0:T(8,128)S(1)} %fusion.14, f32[1,16,10,258]{3,2,1,0:T(8,128)S(1)} %get-tuple-element.15, f32[1,16,10,258]{3,2,1,0:T(8,128)S(1)} %get-tuple-element.16), kind=kLoop, calls=%fused_computation.88 | loop fusion | flops 425984 | bytes 786432 | tf_op jit(solution)/shard_map/sub | solution.py:33
  40.6 5.3 %all-to-all-done.1 = f32[2,8,1024]{2,0,1:T(2,128)S(1)} async-done(((f32[2,8,1024]{2,0,1:T(2,128)}), f32[2,8,1024]{2,0,1:T(2,128)S(1)}, u32[]{:S(2)}, u32[]{:S(2)}) %all-to-all-start.1) | async-done | bytes 65568 | tf_op jit(solution)/shard_map/all_to_all | solution.py:86
  46.3 0.5 copy.71
  47.7 1.2 %copy.74 = f32[2,16,32,64]{3,2,1,0:T(8,128)} copy(f32[2,16,32,64]{2,1,3,0:T(8,128)S(1)} %bitcast.67) | data formatting | bytes 524288
  (34 shorter events, 5.4 us)
Async XLA Ops:
  0.6 7.4 %copy-start = (f32[16,8,256]{2,1,0:T(8,128)S(1)}, f32[16,8,256]{2,1,0:T(8,128)}, u32[]{:S(2)}) copy-start(f32[16,8,256]{2,1,0:T(8,128)} %param.2) | copy-start | bytes 393220
  0.6 7.4 %copy-start.1 = (f32[16,8,256]{2,1,0:T(8,128)S(1)}, f32[16,8,256]{2,1,0:T(8,128)}, u32[]{:S(2)}) copy-start(f32[16,8,256]{2,1,0:T(8,128)} %param.3) | copy-start | bytes 393220
  1.7 5.1 %collective-permute-start = (f32[2,16,8,2]{3,2,1,0:T(8,128)S(1)}, f32[2,16,8,2]{3,2,1,0:T(8,128)S(1)}, u32[]{:S(2)}, u32[]{:S(2)}) collective-permute-start(f32[2,16,8,2]{3,2,1,0:T(8,128)S(1)} %get-tuple-element.27), channel_id=1, source_target_pairs={{0,8},{8,16},{16,24},{24,0},{1,9},{9,17},{17,25},{25,1},{2,10},{10... | collective-permute-start | bytes 6152 | tf_op jit(solution)/shard_map/ppermute | solution.py:19
  2.3 5.8 %collective-permute-start.1 = (f32[2,16,8,2]{3,2,1,0:T(8,128)S(1)}, f32[2,16,8,2]{3,2,1,0:T(8,128)S(1)}, u32[]{:S(2)}, u32[]{:S(2)}) collective-permute-start(f32[2,16,8,2]{3,2,1,0:T(8,128)S(1)} %get-tuple-element.28), channel_id=1, source_target_pairs={{8,0},{16,8},{24,16},{0,24},{9,1},{17,9},{25,17},{1,25},{10,2},{18... | collective-permute-start | bytes 6152 | tf_op jit(solution)/shard_map/ppermute | solution.py:20
  8.4 8.2 %collective-permute-start.2 = (f32[2,16,2,260]{3,2,1,0:T(2,128)S(1)}, f32[2,16,2,260]{3,2,1,0:T(2,128)S(1)}, u32[]{:S(2)}, u32[]{:S(2)}) collective-permute-start(f32[2,16,2,260]{3,2,1,0:T(2,128)S(1)} %get-tuple-element.25), channel_id=1, source_target_pairs={{0,1},{1,2},{2,3},{3,4},{4,5},{5,6},{6,7},{7,0},{8,9},{9,10},{10,1... | collective-permute-start | bytes 199688 | tf_op jit(solution)/shard_map/ppermute | solution.py:19
  10.0 7.7 %collective-permute-start.3 = (f32[2,16,2,260]{3,2,1,0:T(2,128)S(1)}, f32[2,16,2,260]{3,2,1,0:T(2,128)S(1)}, u32[]{:S(2)}, u32[]{:S(2)}) collective-permute-start(f32[2,16,2,260]{3,2,1,0:T(2,128)S(1)} %get-tuple-element.26), channel_id=1, source_target_pairs={{1,0},{2,1},{3,2},{4,3},{5,4},{6,5},{7,6},{0,7},{9,8},{10,9},{11,1... | collective-permute-start | bytes 199688 | tf_op jit(solution)/shard_map/ppermute | solution.py:20
  24.1 11.6 %all-to-all-start = ((f32[2,8,256]{2,0,1:T(2,128)}), f32[2,8,256]{2,0,1:T(2,128)S(1)}, u32[]{:S(2)}, u32[]{:S(2)}) async-start(f32[2,8,256]{2,0,1:T(2,128)} %copy.59), calls=%async_computation | async-start | bytes 32768 | tf_op jit(solution)/shard_map/all_to_all | solution.py:87
  35.7 10.2 %all-to-all-start.1 = ((f32[2,8,1024]{2,0,1:T(2,128)}), f32[2,8,1024]{2,0,1:T(2,128)S(1)}, u32[]{:S(2)}, u32[]{:S(2)}) async-start(f32[2,8,1024]{2,0,1:T(2,128)} %copy.68), calls=%async_computation.1 | async-start | bytes 131072 | tf_op jit(solution)/shard_map/all_to_all | solution.py:86
where the time goes:
time: 49.2 us; the launch traced here: 48.9 us
  waiting for transfers between devices  18.4 us (37%)
  starting transfers between devices  15.6 us (32%)
  local copies, waits for them, and re-layouts  8.57 us (17%)
  other arithmetic  5.44 us (11%)
  between operations  0.88 us (2%)
    ppermute x2, waiting for transfers between devices, with_halo(): before = lax.ppermute(last, axis, up)  5.98 us
    all_to_all x1, waiting for transfers between devices, body(): lax.all_to_all(pack(detail, owners), 'gy', split_axis=1, concat_axis=1, t...  5.34 us
    ppermute x2, starting transfers between devices, with_halo(): after = lax.ppermute(first, axis, down)  5.18 us
    all_to_all x1, starting transfers between devices, body(): lax.all_to_all(pack(level2, owners), 'gy', split_axis=1, concat_axis=1, t...  5 us
    all_to_all x1, waiting for transfers between devices, body(): lax.all_to_all(pack(level2, owners), 'gy', split_axis=1, concat_axis=1, t...  4.71 us
    all_to_all x1, starting transfers between devices, body(): lax.all_to_all(pack(detail, owners), 'gy', split_axis=1, concat_axis=1, t...  3.35 us
    ppermute x2, waiting for transfers between devices, with_halo(): after = lax.ppermute(first, axis, down)  2.34 us
    ppermute x2, starting transfers between devices, with_halo(): before = lax.ppermute(last, axis, up)  2.12 us
  transfers between devices with their start and end apart: 6, of which 6 were waited for; matrix products, arithmetic and copies ran while one was open for 7% of the time, Pallas kernels for 0%

commit v1 on v0

v1 whole, which is shorter than its diff:
```python
import functools

import jax
import jax.numpy as jnp
from jax import lax
from jax.experimental import pallas as pl
from jax.experimental.pallas import tpu as pltpu
from jax.sharding import PartitionSpec as P

feed_rate = 0.037
kill_rate = 0.06
substrate_diffusion = 0.15
catalyst_diffusion = 0.08

MESH = pl.DeviceIdType.MESH
LANES = 128


def react(substrate, catalyst, spread_substrate, spread_catalyst):
    reaction = substrate * catalyst * catalyst
    new_substrate = (
        substrate
        + substrate_diffusion * spread_substrate
        - reaction
        + feed_rate * (1.0 - substrate)
    )
    new_catalyst = (
        catalyst
        + catalyst_diffusion * spread_catalyst
        + reaction
        - (feed_rate + kill_rate) * catalyst
    )
    return new_substrate, new_catalyst


def split(value):
    high = value.astype(jnp.bfloat16)
    low = (value - high.astype(jnp.float32)).astype(jnp.bfloat16)
    return high, low


def spread_of(before, here, after):
    planes, extent = here.shape
    total = pltpu.roll(here, 1, 0) + pltpu.roll(here, planes - 1, 0)
    total = total + before + after
    total = total + pltpu.roll(here, 1, 1) + pltpu.roll(here, extent - 1, 1)
    return total - 6.0 * here


def kernel(dims, fused, *refs):
    planes, columns, extent, owners, slabs_x, slabs_y = dims
    (u_ref, v_ref, u_out, v_out, last_out, loaded, state, edge, packed, got, middle, sums,
     outgoing, incoming, doubled, load_sem, send_sem, recv_sem, deal_send, deal_recv) = refs
    gathered = incoming if fused else last_out
    tiles = extent // LANES
    gx, gy = lax.axis_index("gx"), lax.axis_index("gy")

    barrier = pltpu.get_barrier_semaphore()
    sides = [
        (lax.rem(gx + slabs_x + dx, slabs_x), lax.rem(gy + slabs_y + dy, slabs_y))
        for dx in (-1, 1)
        for dy in (-1, 0, 1)
    ]
    peers = [(gx, lax.rem(gy + step, owners)) for step in range(1, owners)]
    for device in sides + peers:
        pl.semaphore_signal(barrier, inc=1, device_id=device, device_id_type=MESH)

    loads = [
        pltpu.make_async_copy(source, loaded.at[field], load_sem.at[field])
        for field, source in enumerate((u_ref, v_ref))
    ]
    for load in loads:
        load.start()
    for load in loads:
        load.wait()

    lane = lax.broadcasted_iota(jnp.int32, (planes, LANES), 1)
    group = lax.rem(lane + 2, LANES) // 4
    pack = jnp.zeros((planes, LANES), jnp.float32)
    for field in range(2):
        for column in range(columns):
            slab = jnp.concatenate(
                [
                    loaded[field, pl.ds(tile * columns + column, planes, stride=tiles * columns), :]
                    for tile in range(tiles)
                ],
                axis=1,
            )
            state[field, 2 + column] = slab
            at = field * columns + column
            ends = jnp.where(lane < LANES // 2, slab[:, :LANES], slab[:, extent - LANES :])
            ends = pltpu.roll(ends, 4 * at, 1) if at else ends
            pack = jnp.where(group == at, ends, pack)
    packed[...] = pack

    pl.semaphore_wait(barrier, len(sides) + len(peers))

    copies = []
    for side, (target, source) in enumerate(((slice(0, 2), slice(columns, columns + 2)),
                                             (slice(columns + 2, columns + 4), slice(2, 4)))):
        there = lax.rem(gy + (1 if side == 0 else slabs_y - 1), slabs_y)
        copies.append(
            pltpu.make_async_remote_copy(
                src_ref=state.at[:, source],
                dst_ref=state.at[:, target],
                send_sem=send_sem.at[side],
                recv_sem=recv_sem.at[side],
                device_id=(gx, there),
                device_id_type=MESH,
            )
        )
    for number, device in enumerate(sides):
        a, b = (1 - number // 3, 2 - number % 3)
        copies.append(
            pltpu.make_async_remote_copy(
                src_ref=packed,
                dst_ref=got.at[a, b],
                send_sem=send_sem.at[2 + number],
                recv_sem=recv_sem.at[2 + 3 * a + b],
                device_id=device,
                device_id_type=MESH,
            )
        )
    for copy in copies:
        copy.start()

    half = extent // 2
    row = lax.broadcasted_iota(jnp.int32, (half, extent), 0)
    fine = lax.broadcasted_iota(jnp.int32, (half, extent), 1)
    to_blend = jnp.concatenate(
        [
            jnp.where(fine // 2 == row, 0.125, 0.0),
            jnp.where(fine // 4 == row // 2, 0.03125, 0.0),
        ],
        axis=1,
    ).astype(jnp.bfloat16)

    for side in range(2):
        for b in range(3):
            slot = 2 + 3 * side + b
            pltpu.make_async_remote_copy(
                src_ref=packed,
                dst_ref=got.at[side, b],
                send_sem=send_sem.at[slot],
                recv_sem=recv_sem.at[slot],
                device_id=sides[3 * (1 - side) + 2 - b],
                device_id_type=MESH,
            ).wait_recv()
    for side in range(2):
        copies[side].wait_recv()

    both = [jnp.where(lax.rem(lane, 4) < 2, got[1, b], got[0, b]) for b in range(3)]
    for field in range(2):
        for c in range(1, columns + 3):
            if c == 1:
                b, at = 0, field * columns + columns - 1
            elif c == columns + 2:
                b, at = 2, field * columns
            else:
                b, at = 1, field * columns + c - 2
            edge[field, c] = pltpu.roll(both[b], LANES - 4 * at, 1) if at else both[b]

    def wide(field, c):
        if c in (0, columns + 3):
            tail = jnp.zeros((planes, LANES), jnp.float32)
        else:
            tail = edge[field, c]
        return jnp.concatenate([state[field, c], tail], axis=1)

    for c in range(1, columns + 3):
        u, v = wide(0, c), wide(1, c)
        su = spread_of(wide(0, c - 1), u, wide(0, c + 1))
        sv = spread_of(wide(1, c - 1), v, wide(1, c + 1))
        middle[0, c], middle[1, c] = react(u, v, su, sv)

    level = [[], []]
    for c in range(2, columns + 2):
        u, v = middle[0, c], middle[1, c]
        su = spread_of(middle[0, c - 1], u, middle[0, c + 1])
        sv = spread_of(middle[1, c - 1], v, middle[1, c + 1])
        new = react(u[:, :extent], v[:, :extent], su[:, :extent], sv[:, :extent])
        for field, out in enumerate((u_out, v_out)):
            for tile in range(tiles):
                rows = pl.ds(tile * columns + c - 2, planes, stride=tiles * columns)
                out[rows, :] = new[field][:, tile * LANES : (tile + 1) * LANES]
            level[field].append(new[field])

    pairs = columns // 2
    for field in range(2):
        twos = [level[field][2 * k] + level[field][2 * k + 1] for k in range(pairs)]
        fours = [twos[2 * q] + twos[2 * q + 1] for q in range(pairs // 2)]
        for k in range(pairs):
            rows = pl.ds(field * planes * pairs + k, planes, stride=pairs)
            for tile in range(tiles):
                lanes = slice(tile * LANES, (tile + 1) * LANES)
                sums[tile, rows, :] = twos[k][:, lanes]
                sums[tiles + tile, rows, :] = fours[k // 2][:, lanes]

    contract = (((1,), (1,)), ((), ()))
    high, low = split(jnp.concatenate([sums[tile] for tile in range(2 * tiles)], axis=1))
    blend = lax.dot_general(to_blend, high, contract, preferred_element_type=jnp.float32)
    blend += lax.dot_general(to_blend, low, contract, preferred_element_type=jnp.float32)
    portion = half // owners
    for owner in range(owners):
        outgoing[owner] = blend[owner * portion : (owner + 1) * portion]

    deals = []
    for step in range(1, owners):
        deals.append(
            pltpu.make_async_remote_copy(
                src_ref=outgoing.at[lax.rem(gy + step, owners)],
                dst_ref=gathered.at[gy],
                send_sem=deal_send.at[step - 1],
                recv_sem=deal_recv.at[step - 1],
                device_id=(gx, lax.rem(gy + step, owners)),
                device_id_type=MESH,
            )
        )
        deals[-1].start()
    gathered[gy] = outgoing[gy]

    if fused:
        wide_in = lax.broadcasted_iota(jnp.int32, (LANES, 4 * LANES), 0)
        wide_out = lax.broadcasted_iota(jnp.int32, (LANES, 4 * LANES), 1)
        column_of = wide_in // 16 * 4 + wide_in % 4
        spreading = jnp.where(
            (wide_in // 4 % 4 == wide_out // LANES) & (column_of == wide_out % LANES // 2),
            1.0,
            0.0,
        ).astype(jnp.bfloat16)
        lane = lax.broadcasted_iota(jnp.int32, (portion, LANES), 1)

    for deal in deals:
        deal.wait_recv()

    if fused:
        blocks = [incoming[owner] for owner in range(owners)]
        for h in range(8):
            part = jnp.zeros((portion, LANES), jnp.float32)
            for owner in range(8):
                shift = (16 * (owner - h)) % LANES
                moved = pltpu.roll(blocks[owner], shift, 1) if shift else blocks[owner]
                part = jnp.where(lane // 16 == owner, moved, part)
            doubled[pl.ds(2 * h * portion, portion, stride=2), :] = part
            doubled[pl.ds(2 * h * portion + 1, portion, stride=2), :] = part
        high, low = split(doubled[...])
        whole = jnp.dot(high, spreading, preferred_element_type=jnp.float32)
        whole += jnp.dot(low, spreading, preferred_element_type=jnp.float32)
        width, rows = last_out.shape[1], 2 * portion
        for h in range(8):
            for z in range(4):
                base = (h * 4 + z) * rows
                last_out[base : base + rows, :] = whole[
                    h * rows : (h + 1) * rows, z * LANES : z * LANES + width
                ]

    for copy in copies:
        copy.wait_send()
    for deal in deals:
        deal.wait_send()


def tiled(field):
    planes, columns, extent = field.shape
    field = field.reshape(planes, columns, extent // LANES, LANES)
    return jnp.transpose(field, (0, 2, 1, 3)).reshape(-1, LANES)


def untiled(field, shape):
    planes, columns, extent = shape
    field = field.reshape(planes, extent // LANES, columns, LANES)
    return jnp.transpose(field, (0, 2, 1, 3)).reshape(shape)


def body(substrate, catalyst):
    planes, columns, extent = substrate.shape
    slabs_x, owners = lax.axis_size("gx"), lax.axis_size("gy")
    half, pairs, tiles = extent // 2, columns // 2, extent // LANES
    portion = half // owners
    values = 2 * planes * pairs
    fused = (
        planes == 16 and pairs == 4 and owners == 8 and values == LANES and portion % 8 == 0
    )
    dims = (planes, columns, extent, owners, slabs_x, owners)
    flat = jax.ShapeDtypeStruct((planes * tiles * columns, LANES), jnp.float32)
    dealt = jax.ShapeDtypeStruct((owners, portion, values), jnp.float32)
    rebuilt_rows = 2 * portion
    last = (
        jax.ShapeDtypeStruct((2 * planes * rebuilt_rows, columns * owners), jnp.float32)
        if fused
        else dealt
    )
    vmem = pl.BlockSpec(memory_space=pltpu.VMEM)
    f32 = jnp.float32
    u, v, final = pl.pallas_call(
        functools.partial(kernel, dims, fused),
        out_shape=(flat, flat, last),
        in_specs=[pl.BlockSpec(memory_space=pl.ANY)] * 2,
        out_specs=(vmem, vmem, vmem),
        scratch_shapes=[
            pltpu.VMEM((2, planes * tiles * columns, LANES), f32),
            pltpu.VMEM((2, columns + 4, planes, extent), f32),
            pltpu.VMEM((2, columns + 4, planes, LANES), f32),
            pltpu.VMEM((planes, LANES), f32),
            pltpu.VMEM((2, 3, planes, LANES), f32),
            pltpu.VMEM((2, columns + 4, planes, extent + LANES), f32),
            pltpu.VMEM((2 * tiles, values, LANES), f32),
            pltpu.VMEM((owners, portion, values), f32),
            pltpu.VMEM((owners, portion, values) if fused else (8, LANES), f32),
            pltpu.VMEM((16 * portion, LANES), f32),
            pltpu.SemaphoreType.DMA((2,)),
            pltpu.SemaphoreType.DMA((8,)),
            pltpu.SemaphoreType.DMA((8,)),
            pltpu.SemaphoreType.DMA((owners - 1,)),
            pltpu.SemaphoreType.DMA((owners - 1,)),
        ],
        compiler_params=pltpu.CompilerParams(collective_id=0, has_side_effects=True),
    )(
        tiled(substrate),
        tiled(catalyst),
    )
    if fused:
        rebuilt = final.reshape(2, planes, rebuilt_rows, columns * owners)
    else:
        blend = final.reshape(owners, portion, 2, planes, pairs)
        blend = jnp.transpose(blend, (2, 3, 1, 0, 4)).reshape(2, planes, portion, owners * pairs)
        rebuilt = jnp.repeat(jnp.repeat(blend, 2, axis=2), 2, axis=3)
    return untiled(u, substrate.shape), untiled(v, substrate.shape), rebuilt


def solution(mesh):
    in_specs = (P(None, "gy", "gx"), P(None, "gy", "gx"))
    out_specs = (P(None, "gy", "gx"), P(None, "gy", "gx"), P(None, None, ("gx", "gy"), None))
    return jax.shard_map(body, mesh=mesh, in_specs=in_specs, out_specs=out_specs, check_vma=False)
```

time: 49.2 us -> 23.4 us (0.48)
  Pallas kernels: 0 us -> 18.6 us
  waiting for transfers between devices: 18.4 us -> 0 us
  starting transfers between devices: 15.6 us -> 0 us
  other arithmetic: 5.44 us -> 0 us
  local copies, waits for them, and re-layouts: 8.57 us -> 3.99 us
    pallas_call x0 -> x1, Pallas kernels: none -> 18.6 us  [body(): pl.pallas_call(functools.partial(kernel, dims, fused), out_shape=(flat, f...]
    all_to_all x2 -> x0, waiting for transfers between devices: 10 us -> none  [the longest x1 5.34 us: body(): lax.all_to_all(pack(detail, owners), 'gy', split_axis=1, concat_axis=1, t...]
    all_to_all x2 -> x0, starting transfers between devices: 8.35 us -> none  [the longest x1 5 us: body(): lax.all_to_all(pack(level2, owners), 'gy', split_axis=1, concat_axis=1, t...]
    ppermute x4 -> x0, waiting for transfers between devices: 8.33 us -> none  [the longest x2 5.98 us: with_halo(): before = lax.ppermute(last, axis, up)]
    ppermute x4 -> x0, starting transfers between devices: 7.3 us -> none  [the longest x2 5.18 us: with_halo(): after = lax.ppermute(first, axis, down)]
    sub x5 -> x0, other arithmetic: 2.93 us -> none  [the longest x2 1.65 us: advance(): return react(center, spread - 6.0 * center)]
    unnamed x5, local copies, waits for them, and re-layouts: 1.23 us -> 3.99 us
    reshape x6 -> x0, local copies, waits for them, and re-layouts: 2.51 us -> none  [the longest x2 1.64 us: pack(): return blocks.reshape(fields, owners, planes * portion * extent)]
  transfers between devices with their start and end apart: 6 -> 0, of which waited for: 6 -> 0; matrix products, arithmetic and copies ran while one was open for 7% -> 0% of each run, Pallas kernels for 0% -> 0%
where the time goes in v1:
time: 23.4 us; the launch traced here: 23.2 us
  Pallas kernels  18.6 us (79%)
  local copies, waits for them, and re-layouts  3.99 us (17%)
  between operations  0.65 us (3%)
    pallas_call x1, Pallas kernels, body(): pl.pallas_call(functools.partial(kernel, dims, fused), out_shape=(flat, f...  18.6 us
    unnamed x5, local copies, waits for them, and re-layouts  3.99 us

profile of v1, /device:TPU:0, one launch (start us, length us, event | category | flops | bytes accessed | tf_op | source)
XLA Modules:
  0.0 23.2 jit_solution(17308956758493608905)
XLA Ops:
  0.6 18.6 %shard_map.49 = (f32[256,128]{1,0:T(8,128)}, f32[256,128]{1,0:T(8,128)}, f32[1024,64]{1,0:T(8,128)}) custom-call(f32[256,128]{1,0:T(8,128)} %bitcast.22, f32[256,128]{1,0:T(8,128)} %bitcast.23), custom_call_target="tpu_custom_call" | custom-call | tf_op jit(solution)/shard_map/pallas_call | solution.py:295
  19.2 0.0 copy-start
  19.3 1.6 %copy.8 = f32[16,8,256]{2,1,0:T(8,128)} copy(f32[16,8,256]{2,1,0:T(8,128)} %bitcast.25) | data formatting | bytes 262144
  20.9 1.6 %copy.9 = f32[16,8,256]{2,1,0:T(8,128)} copy(f32[16,8,256]{2,1,0:T(8,128)} %bitcast.24) | data formatting | bytes 262144
  22.4 0.0 copy-done
  22.5 0.8 %copy.10 = f32[2,16,32,64]{3,2,1,0:T(8,128)} copy(f32[2,16,32,64]{3,2,1,0:T(8,128)S(1)} %bitcast.21) | data formatting | bytes 524288
Async XLA Ops:
  19.2 3.2 %copy-start = (f32[1024,64]{1,0:T(8,128)S(1)}, f32[1024,64]{1,0:T(8,128)}, u32[]{:S(2)}) copy-start(f32[1024,64]{1,0:T(8,128)} %get-tuple-element.8) | copy-start | bytes 786436

commit v2 on v1

--- a/solution.py
+++ b/solution.py
@@ -47,11 +47,10 @@
     return total - 6.0 * here
 
 
-def kernel(dims, fused, *refs):
+def kernel(dims, *refs):
     planes, columns, extent, owners, slabs_x, slabs_y = dims
-    (u_ref, v_ref, u_out, v_out, last_out, loaded, state, edge, packed, got, middle, sums,
-     outgoing, incoming, doubled, load_sem, send_sem, recv_sem, deal_send, deal_recv) = refs
-    gathered = incoming if fused else last_out
+    (u_ref, v_ref, u_out, v_out, gathered, loaded, state, edge, packed, got, middle, sums,
+     outgoing, load_sem, send_sem, recv_sem, deal_send, deal_recv) = refs
     tiles = extent // LANES
     gx, gy = lax.axis_index("gx"), lax.axis_index("gy")
 
@@ -219,45 +218,66 @@
         deals[-1].start()
     gathered[gy] = outgoing[gy]
 
-    if fused:
-        wide_in = lax.broadcasted_iota(jnp.int32, (LANES, 4 * LANES), 0)
-        wide_out = lax.broadcasted_iota(jnp.int32, (LANES, 4 * LANES), 1)
-        column_of = wide_in // 16 * 4 + wide_in % 4
-        spreading = jnp.where(
-            (wide_in // 4 % 4 == wide_out // LANES) & (column_of == wide_out % LANES // 2),
-            1.0,
-            0.0,
-        ).astype(jnp.bfloat16)
-        lane = lax.broadcasted_iota(jnp.int32, (portion, LANES), 1)
-
     for deal in deals:
         deal.wait_recv()
 
-    if fused:
-        blocks = [incoming[owner] for owner in range(owners)]
-        for h in range(8):
+    for copy in copies:
+        copy.wait_send()
+    for deal in deals:
+        deal.wait_send()
+
+
+def finish(u_ref, v_ref, dealt, u_out, v_out, rebuilt_out, doubled, rebuilt, sems):
+    copies = [
+        pltpu.make_async_copy(u_ref, u_out, sems.at[0]),
+        pltpu.make_async_copy(v_ref, v_out, sems.at[1]),
+    ]
+    for copy in copies:
+        copy.start()
+
+    owners, portion, _ = dealt.shape
+    wide_in = lax.broadcasted_iota(jnp.int32, (LANES, 4 * LANES), 0)
+    wide_out = lax.broadcasted_iota(jnp.int32, (LANES, 4 * LANES), 1)
+    column_of = wide_in // 16 * 4 + wide_in % 4
+    spreading = jnp.where(
+        (wide_in // 4 % 4 == wide_out // LANES) & (column_of == wide_out % LANES // 2),
+        1.0,
+        0.0,
+    ).astype(jnp.bfloat16)
+    lane = lax.broadcasted_iota(jnp.int32, (portion, LANES), 1)
+    blocks = [dealt[owner] for owner in range(owners)]
+    width, rows = rebuilt.shape[1], 2 * portion
+    chunks = 4
+    share = 8 // chunks
+    for chunk in range(chunks):
+        for h in range(chunk * share, (chunk + 1) * share):
             part = jnp.zeros((portion, LANES), jnp.float32)
             for owner in range(8):
                 shift = (16 * (owner - h)) % LANES
                 moved = pltpu.roll(blocks[owner], shift, 1) if shift else blocks[owner]
                 part = jnp.where(lane // 16 == owner, moved, part)
-            doubled[pl.ds(2 * h * portion, portion, stride=2), :] = part
-            doubled[pl.ds(2 * h * portion + 1, portion, stride=2), :] = part
-        high, low = split(doubled[...])
+            doubled[pl.ds(h * rows, portion, stride=2), :] = part
+            doubled[pl.ds(h * rows + 1, portion, stride=2), :] = part
+        high, low = split(doubled[chunk * share * rows : (chunk + 1) * share * rows, :])
         whole = jnp.dot(high, spreading, preferred_element_type=jnp.float32)
         whole += jnp.dot(low, spreading, preferred_element_type=jnp.float32)
-        width, rows = last_out.shape[1], 2 * portion
-        for h in range(8):
+        for h in range(share):
             for z in range(4):
-                base = (h * 4 + z) * rows
-                last_out[base : base + rows, :] = whole[
+                base = ((chunk * share + h) * 4 + z) * rows
+                rebuilt[base : base + rows, :] = whole[
                     h * rows : (h + 1) * rows, z * LANES : z * LANES + width
                 ]
-
+        size = share * 4 * rows
+        copies.append(
+            pltpu.make_async_copy(
+                rebuilt.at[chunk * size : (chunk + 1) * size],
+                rebuilt_out.at[chunk * size : (chunk + 1) * size],
+                sems.at[2 + chunk],
+            )
+        )
+        copies[-1].start()
     for copy in copies:
-        copy.wait_send()
-    for deal in deals:
-        deal.wait_send()
+        copy.wait()
 
 
 def tiled(field):
@@ -282,23 +302,21 @@
         planes == 16 and pairs == 4 and owners == 8 and values == LANES and portion % 8 == 0
     )
     dims = (planes, columns, extent, owners, slabs_x, owners)
-    flat = jax.ShapeDtypeStruct((planes * tiles * columns, LANES), jnp.float32)
-    dealt = jax.ShapeDtypeStruct((owners, portion, values), jnp.float32)
-    rebuilt_rows = 2 * portion
-    last = (
-        jax.ShapeDtypeStruct((2 * planes * rebuilt_rows, columns * owners), jnp.float32)
-        if fused
-        else dealt
-    )
+    f32 = jnp.float32
+    flat = (planes * tiles * columns, LANES)
     vmem = pl.BlockSpec(memory_space=pltpu.VMEM)
-    f32 = jnp.float32
-    u, v, final = pl.pallas_call(
-        functools.partial(kernel, dims, fused),
-        out_shape=(flat, flat, last),
-        in_specs=[pl.BlockSpec(memory_space=pl.ANY)] * 2,
-        out_specs=(vmem, vmem, vmem),
+    anywhere = pl.BlockSpec(memory_space=pl.ANY)
+    u, v, dealt = pl.pallas_call(
+        functools.partial(kernel, dims),
+        out_shape=(
+            pltpu.VMEM(flat, f32),
+            pltpu.VMEM(flat, f32),
+            pltpu.VMEM((owners, portion, values), f32),
+        ),
+        in_specs=[anywhere] * 2,
+        out_specs=(vmem,) * 3,
         scratch_shapes=[
-            pltpu.VMEM((2, planes * tiles * columns, LANES), f32),
+            pltpu.VMEM((2,) + flat, f32),
             pltpu.VMEM((2, columns + 4, planes, extent), f32),
             pltpu.VMEM((2, columns + 4, planes, LANES), f32),
             pltpu.VMEM((planes, LANES), f32),
@@ -306,8 +324,6 @@
             pltpu.VMEM((2, columns + 4, planes, extent + LANES), f32),
             pltpu.VMEM((2 * tiles, values, LANES), f32),
             pltpu.VMEM((owners, portion, values), f32),
-            pltpu.VMEM((owners, portion, values) if fused else (8, LANES), f32),
-            pltpu.VMEM((16 * portion, LANES), f32),
             pltpu.SemaphoreType.DMA((2,)),
             pltpu.SemaphoreType.DMA((8,)),
             pltpu.SemaphoreType.DMA((8,)),
@@ -315,14 +331,30 @@
             pltpu.SemaphoreType.DMA((owners - 1,)),
         ],
         compiler_params=pltpu.CompilerParams(collective_id=0, has_side_effects=True),
-    )(
-        tiled(substrate),
-        tiled(catalyst),
-    )
+    )(tiled(substrate), tiled(catalyst))
+    rows, width = 2 * portion, columns * owners
     if fused:
-        rebuilt = final.reshape(2, planes, rebuilt_rows, columns * owners)
+        u, v, dealt = (
+            pltpu.with_memory_space_constraint(x, pltpu.VMEM) for x in (u, v, dealt)
+        )
+        u, v, rebuilt = pl.pallas_call(
+            finish,
+            out_shape=(
+                jax.ShapeDtypeStruct(flat, f32),
+                jax.ShapeDtypeStruct(flat, f32),
+                jax.ShapeDtypeStruct((2 * planes * rows, width), f32),
+            ),
+            in_specs=[vmem] * 3,
+            out_specs=(anywhere,) * 3,
+            scratch_shapes=[
+                pltpu.VMEM((8 * rows, LANES), f32),
+                pltpu.VMEM((2 * planes * rows, width), f32),
+                pltpu.SemaphoreType.DMA((6,)),
+            ],
+        )(u, v, dealt)
+        rebuilt = rebuilt.reshape(2, planes, rows, width)
     else:
-        blend = final.reshape(owners, portion, 2, planes, pairs)
+        blend = dealt.reshape(owners, portion, 2, planes, pairs)
         blend = jnp.transpose(blend, (2, 3, 1, 0, 4)).reshape(2, planes, portion, owners * pairs)
         rebuilt = jnp.repeat(jnp.repeat(blend, 2, axis=2), 2, axis=3)
     return untiled(u, substrate.shape), untiled(v, substrate.shape), rebuilt

time: 23.4 us -> 19.1 us (0.82)
  local copies, waits for them, and re-layouts: 3.99 us -> 0 us
  Pallas kernels: 18.6 us -> 18.3 us
    unnamed x5 -> x0, local copies, waits for them, and re-layouts: 3.99 us -> none
    pallas_call x1 -> x2, Pallas kernels: 18.6 us -> 18.3 us  [the longest x1 17.2 us: body(): pl.pallas_call(functools.partial(kernel, dims), out_shape=(pltpu.VMEM(fla...]
where the time goes in v2:
time: 19.1 us; the launch traced here: 18.9 us
  Pallas kernels  18.3 us (96%)
  between operations  0.64 us (3%)
    pallas_call x1, Pallas kernels, body(): pl.pallas_call(functools.partial(kernel, dims), out_shape=(pltpu.VMEM(fla...  17.2 us
    pallas_call x1, Pallas kernels, body(): pl.pallas_call(finish, out_shape=(jax.ShapeDtypeStruct(flat, f32), jax.Sh...  1.1 us

profile of v2, /device:TPU:0, one launch (start us, length us, event | category | flops | bytes accessed | tf_op | source)
XLA Modules:
  0.0 18.9 jit_solution(10806199072660014283)
XLA Ops:
  0.6 17.2 %shard_map.49 = (f32[256,128]{1,0:T(8,128)S(1)}, f32[256,128]{1,0:T(8,128)S(1)}, f32[8,16,128]{2,1,0:T(8,128)S(1)}) custom-call(f32[256,128]{1,0:T(8,128)} %bitcast.21, f32[256,128]{1,0:T(8,128)} %bitcast.22), custom_call_target="tpu_custom_call" | custom-call | tf_op jit(solution)/shard_map/pallas_call | solution.py:309
  17.8 1.1 %shard_map.50 = (f32[256,128]{1,0:T(8,128)}, f32[256,128]{1,0:T(8,128)}, f32[1024,64]{1,0:T(8,128)}) custom-call(f32[256,128]{1,0:T(8,128)S(1)} %get-tuple-element.9.u_ref, f32[256,128]{1,0:T(8,128)S(1)} %get-tuple-element.10.v_ref, f32[8,16,128]{2,1,0:T(8,128)S(1)} %get-tuple-element.11.dealt), custom_call_target="tpu_custom_call" | custom-call | tf_op jit(solution)/shard_map/pallas_call | solution.py:340

commit v3 on v2

--- a/solution.py
+++ b/solution.py
@@ -47,19 +47,26 @@
     return total - 6.0 * here
 
 
+def partner_of(me, step, size):
+    if size & (size - 1):
+        return lax.rem(me + step, size)
+    partner = me + step
+    for bit in range(size.bit_length() - 1):
+        if step >> bit & 1:
+            partner = partner - 2 * (1 << bit) * lax.rem(me // (1 << bit), 2)
+    return partner
+
+
 def kernel(dims, *refs):
     planes, columns, extent, owners, slabs_x, slabs_y = dims
-    (u_ref, v_ref, u_out, v_out, gathered, loaded, state, edge, packed, got, middle, sums,
+    (u_ref, v_ref, u_out, v_out, gathered, loaded, state, edge, packed, got, relay, relayed, middle, sums,
      outgoing, load_sem, send_sem, recv_sem, deal_send, deal_recv) = refs
     tiles = extent // LANES
     gx, gy = lax.axis_index("gx"), lax.axis_index("gy")
 
     barrier = pltpu.get_barrier_semaphore()
-    sides = [
-        (lax.rem(gx + slabs_x + dx, slabs_x), lax.rem(gy + slabs_y + dy, slabs_y))
-        for dx in (-1, 1)
-        for dy in (-1, 0, 1)
-    ]
+    sides = [(lax.rem(gx + shift, slabs_x), gy) for shift in (1, slabs_x - 1)]
+    ends = [(gx, lax.rem(gy + shift, owners)) for shift in (1, owners - 1)]
     peers = [(gx, lax.rem(gy + step, owners)) for step in range(1, owners)]
     for device in sides + peers:
         pl.semaphore_signal(barrier, inc=1, device_id=device, device_id_type=MESH)
@@ -87,40 +94,31 @@
             )
             state[field, 2 + column] = slab
             at = field * columns + column
-            ends = jnp.where(lane < LANES // 2, slab[:, :LANES], slab[:, extent - LANES :])
-            ends = pltpu.roll(ends, 4 * at, 1) if at else ends
-            pack = jnp.where(group == at, ends, pack)
+            tips = jnp.where(lane < LANES // 2, slab[:, :LANES], slab[:, extent - LANES :])
+            tips = pltpu.roll(tips, 4 * at, 1) if at else tips
+            pack = jnp.where(group == at, tips, pack)
     packed[...] = pack
 
     pl.semaphore_wait(barrier, len(sides) + len(peers))
 
-    copies = []
-    for side, (target, source) in enumerate(((slice(0, 2), slice(columns, columns + 2)),
-                                             (slice(columns + 2, columns + 4), slice(2, 4)))):
-        there = lax.rem(gy + (1 if side == 0 else slabs_y - 1), slabs_y)
-        copies.append(
-            pltpu.make_async_remote_copy(
-                src_ref=state.at[:, source],
-                dst_ref=state.at[:, target],
-                send_sem=send_sem.at[side],
-                recv_sem=recv_sem.at[side],
-                device_id=(gx, there),
-                device_id_type=MESH,
-            )
+    def send(number, source, target, device):
+        return pltpu.make_async_remote_copy(
+            src_ref=source,
+            dst_ref=target,
+            send_sem=send_sem.at[number],
+            recv_sem=recv_sem.at[number],
+            device_id=device,
+            device_id_type=MESH,
         )
-    for number, device in enumerate(sides):
-        a, b = (1 - number // 3, 2 - number % 3)
-        copies.append(
-            pltpu.make_async_remote_copy(
-                src_ref=packed,
-                dst_ref=got.at[a, b],
-                send_sem=send_sem.at[2 + number],
-                recv_sem=recv_sem.at[2 + 3 * a + b],
-                device_id=device,
-                device_id_type=MESH,
-            )
-        )
-    for copy in copies:
+
+    low_end, high_end = slice(0, 2), slice(columns + 2, columns + 4)
+    across = [send(2 + side, packed, got.at[side], sides[side]) for side in range(2)]
+    along = [
+        send(0, state.at[:, columns : columns + 2], state.at[:, low_end], ends[0]),
+        send(1, state.at[:, 2:4], state.at[:, high_end], ends[1]),
+    ]
+    corners = [send(4 + side, relay, relayed.at[side], ends[side]) for side in range(2)]
+    for copy in across + along:
         copy.start()
 
     half = extent // 2
@@ -134,30 +132,21 @@
         axis=1,
     ).astype(jnp.bfloat16)
 
-    for side in range(2):
-        for b in range(3):
-            slot = 2 + 3 * side + b
-            pltpu.make_async_remote_copy(
-                src_ref=packed,
-                dst_ref=got.at[side, b],
-                send_sem=send_sem.at[slot],
-                recv_sem=recv_sem.at[slot],
-                device_id=sides[3 * (1 - side) + 2 - b],
-                device_id_type=MESH,
-            ).wait_recv()
-    for side in range(2):
-        copies[side].wait_recv()
-
-    both = [jnp.where(lax.rem(lane, 4) < 2, got[1, b], got[0, b]) for b in range(3)]
+    for copy in across:
+        copy.wait_recv()
+
+    both = jnp.where(lax.rem(lane, 4) < 2, got[1], got[0])
+    relay[...] = both
+
+    def place(field, c, tile, column):
+        at = field * columns + column
+        edge[field, c] = pltpu.roll(tile, LANES - 4 * at, 1) if at else tile
+
     for field in range(2):
-        for c in range(1, columns + 3):
-            if c == 1:
-                b, at = 0, field * columns + columns - 1
-            elif c == columns + 2:
-                b, at = 2, field * columns
-            else:
-                b, at = 1, field * columns + c - 2
-            edge[field, c] = pltpu.roll(both[b], LANES - 4 * at, 1) if at else both[b]
+        for c in range(2, columns + 2):
+            place(field, c, both, c - 2)
+    for copy in corners:
+        copy.start()
 
     def wide(field, c):
         if c in (0, columns + 3):
@@ -166,14 +155,15 @@
             tail = edge[field, c]
         return jnp.concatenate([state[field, c], tail], axis=1)
 
-    for c in range(1, columns + 3):
+    def first(c):
         u, v = wide(0, c), wide(1, c)
         su = spread_of(wide(0, c - 1), u, wide(0, c + 1))
         sv = spread_of(wide(1, c - 1), v, wide(1, c + 1))
         middle[0, c], middle[1, c] = react(u, v, su, sv)
 
-    level = [[], []]
-    for c in range(2, columns + 2):
+    level = [{}, {}]
+
+    def second(c):
         u, v = middle[0, c], middle[1, c]
         su = spread_of(middle[0, c - 1], u, middle[0, c + 1])
         sv = spread_of(middle[1, c - 1], v, middle[1, c + 1])
@@ -182,7 +172,23 @@
             for tile in range(tiles):
                 rows = pl.ds(tile * columns + c - 2, planes, stride=tiles * columns)
                 out[rows, :] = new[field][:, tile * LANES : (tile + 1) * LANES]
-            level[field].append(new[field])
+            level[field][c - 2] = new[field]
+
+    for c in range(3, columns + 1):
+        first(c)
+    for c in range(4, columns):
+        second(c)
+    for side, (outer, steps, last) in enumerate(
+        ((1, (1, 2), (2, 3)), (columns + 2, (columns + 2, columns + 1), (columns + 1, columns)))
+    ):
+        along[side].wait_recv()
+        corners[side].wait_recv()
+        for field in range(2):
+            place(field, outer, relayed[side], (1 - side) * (columns - 1))
+        for c in steps:
+            first(c)
+        for c in last:
+            second(c)
 
     pairs = columns // 2
     for field in range(2):
@@ -204,14 +210,15 @@
         outgoing[owner] = blend[owner * portion : (owner + 1) * portion]
 
     deals = []
-    for step in range(1, owners):
+    for step in range(owners - 1, 0, -1):
+        partner = partner_of(gy, step, owners)
         deals.append(
             pltpu.make_async_remote_copy(
-                src_ref=outgoing.at[lax.rem(gy + step, owners)],
+                src_ref=outgoing.at[partner],
                 dst_ref=gathered.at[gy],
                 send_sem=deal_send.at[step - 1],
                 recv_sem=deal_recv.at[step - 1],
-                device_id=(gx, lax.rem(gy + step, owners)),
+                device_id=(gx, partner),
                 device_id_type=MESH,
             )
         )
@@ -221,7 +228,7 @@
     for deal in deals:
         deal.wait_recv()
 
-    for copy in copies:
+    for copy in across + along + corners:
         copy.wait_send()
     for deal in deals:
         deal.wait_send()
@@ -320,13 +327,15 @@
             pltpu.VMEM((2, columns + 4, planes, extent), f32),
             pltpu.VMEM((2, columns + 4, planes, LANES), f32),
             pltpu.VMEM((planes, LANES), f32),
-            pltpu.VMEM((2, 3, planes, LANES), f32),
+            pltpu.VMEM((2, planes, LANES), f32),
+            pltpu.VMEM((planes, LANES), f32),
+            pltpu.VMEM((2, planes, LANES), f32),
             pltpu.VMEM((2, columns + 4, planes, extent + LANES), f32),
             pltpu.VMEM((2 * tiles, values, LANES), f32),
             pltpu.VMEM((owners, portion, values), f32),
             pltpu.SemaphoreType.DMA((2,)),
-            pltpu.SemaphoreType.DMA((8,)),
-            pltpu.SemaphoreType.DMA((8,)),
+            pltpu.SemaphoreType.DMA((6,)),
+            pltpu.SemaphoreType.DMA((6,)),
             pltpu.SemaphoreType.DMA((owners - 1,)),
             pltpu.SemaphoreType.DMA((owners - 1,)),
         ],

time: 19.1 us -> 18.8 us (0.984)
  Pallas kernels: 18.3 us -> 18 us
    pallas_call x1, Pallas kernels: 17.2 us -> 16.9 us  [body(): pl.pallas_call(functools.partial(kernel, dims), out_shape=(pltpu.VMEM(fla...]
where the time goes in v3:
time: 18.8 us; the launch traced here: 18.6 us
  Pallas kernels  18 us (96%)
  between operations  0.64 us (3%)
    pallas_call x1, Pallas kernels, body(): pl.pallas_call(functools.partial(kernel, dims), out_shape=(pltpu.VMEM(fla...  16.9 us
    pallas_call x1, Pallas kernels, body(): pl.pallas_call(finish, out_shape=(jax.ShapeDtypeStruct(flat, f32), jax.Sh...  1.11 us

profile of v3, /device:TPU:0, one launch (start us, length us, event | category | flops | bytes accessed | tf_op | source)
XLA Modules:
  0.0 18.6 jit_solution(24565508153213263)
XLA Ops:
  0.6 16.9 %shard_map.49 = (f32[256,128]{1,0:T(8,128)S(1)}, f32[256,128]{1,0:T(8,128)S(1)}, f32[8,16,128]{2,1,0:T(8,128)S(1)}) custom-call(f32[256,128]{1,0:T(8,128)} %bitcast.21, f32[256,128]{1,0:T(8,128)} %bitcast.22), custom_call_target="tpu_custom_call" | custom-call | tf_op jit(solution)/shard_map/pallas_call | solution.py:316
  17.5 1.1 %shard_map.50 = (f32[256,128]{1,0:T(8,128)}, f32[256,128]{1,0:T(8,128)}, f32[1024,64]{1,0:T(8,128)}) custom-call(f32[256,128]{1,0:T(8,128)S(1)} %get-tuple-element.9.u_ref, f32[256,128]{1,0:T(8,128)S(1)} %get-tuple-element.10.v_ref, f32[8,16,128]{2,1,0:T(8,128)S(1)} %get-tuple-element.11.dealt), custom_call_target="tpu_custom_call" | custom-call | tf_op jit(solution)/shard_map/pallas_call | solution.py:349
